TPU v7x, 256 devices: a whole 4x4x8 slice. The times are simulated.
256 devices in a mesh: cp: 64 (over z_hi, y, x, core), tp: 4 (over z_lo).
Axes of the slice: x: 4, y: 4, z: 8 (z_hi: 2, z_lo: 4; z = z_hi * 4 + z_lo), core: 2. Of those that a mesh axis runs over, the one named last changes fastest.
Arguments:
- queries: bfloat16 [49152, 5120], P('cp', 'tp'), may hold values from -36 to 36
- keys: bfloat16 [49152, 1024], P('cp', 'tp'), may hold values from -5 to 5
- values: bfloat16 [49152, 1024], P('cp', 'tp'), may hold values from -6 to 6
- doc_lengths: int32 [64], replicated, may hold values from 1 to 1536, 49152 in all
Outputs:
- attended: bfloat16 [49152, 5120], P(('cp', 'tp'))
Inputs may be any that keep to these rules, and one draw needn't show every extreme that they name: `doc_lengths`: they sum to 49152, and one of them is exactly 1536.
All inputs are finite; a program needn't handle non-finite values.
Results may differ from a plain program's by a relative error of at most 0.0038.
Values may be sent and summed in bfloat16 or wider, within the bound.
No kernel may reach another device: no remote copies, remote signals or barrier semaphores. Data moves between devices by JAX's collectives and lax.ppermute only.
A program may use at most 256 MiB of HBM per device.

v0:
```python
import functools

import jax
import jax.numpy as jnp
from jax import lax
from jax.experimental import pallas as pl
from jax.experimental.pallas import tpu as pltpu
from jax.sharding import PartitionSpec as P


HEAD = 128
TILE = 256
negative = -1e30
factor = float(HEAD) ** (-0.5) * 1.4426950408889634


anywhere = pl.BlockSpec(memory_space=pltpu.HBM)
scalars = pl.BlockSpec(memory_space=pltpu.SMEM)
fast = pl.BlockSpec(memory_space=pltpu.VMEM)


def device_of(stretch, cp_size):
    if stretch < cp_size // 2:
        return 2 * stretch
    return 2 * (cp_size - 1 - stretch) + 1


def run_all(copies):
    for copy in copies:
        copy.start()
    for copy in copies:
        copy.wait()


def join_kernel(half, heads, bounds, k_ref, v_ref, k_got, v_got, *rest):
    del bounds
    outs, sems = rest[:heads], rest[heads]
    mine = pl.ds(pl.multiple_of((lax.axis_index("cp") % 2) * half, half), half)
    copies = []
    for h in range(heads):
        cols = slice(h * HEAD, (h + 1) * HEAD)
        for n, (own, got) in enumerate(((k_ref, k_got), (v_ref, v_got))):
            first = 2 * half * n
            copies.append((own.at[mine, cols], outs[h].at[pl.ds(first, half), :]))
            copies.append((got.at[mine, cols], outs[h].at[pl.ds(first + half, half), :]))
    run_all([pltpu.make_async_copy(a, b, sems.at[i]) for i, (a, b) in enumerate(copies)])


def join(bounds, keys, values, k_got, v_got):
    rows, cols = keys.shape
    heads = cols // HEAD
    return pl.pallas_call(
        functools.partial(join_kernel, rows // 2, heads),
        in_specs=[scalars, anywhere, anywhere, fast, fast],
        out_specs=[fast] * heads,
        out_shape=[jax.ShapeDtypeStruct((2 * rows, HEAD), keys.dtype)] * heads,
        scratch_shapes=[pltpu.SemaphoreType.DMA((4 * heads,))],
        compiler_params=pltpu.CompilerParams(vmem_limit_bytes=4 << 20),
    )(bounds, keys, values, k_got, v_got)


def attend_kernel(head, low, high, opening, closing, pieces, cp_size, far_stretches, *refs):
    refs = list(refs)
    take = lambda n: [refs.pop(0) for _ in range(n)]
    bounds, starts = take(2)
    me = lax.axis_index("cp")
    my_tp = lax.axis_index("tp")
    stretches = high // 3 - low // 3
    q_ref, q_got = take(2) if opening else (None, None)
    far = take(1)[0] if low == 0 else None
    messages = take(stretches)
    if not opening:
        take(4)
    outs = take(pieces) if closing else []
    qbuf, m_ref, l_ref, acc_ref = take(4)
    kbuf, vbuf, keep_ref, s_ref, p_ref, bias_ref, item_t, item_k, item_m = take(9)
    obuf = take(1)[0] if closing else None
    sems = take(1)[0]

    rows, cols = qbuf.shape
    half = rows // 2
    tiles = rows // TILE
    group = cols // HEAD
    base = 2 * tiles

    if opening:
        mine = pl.ds(pl.multiple_of((me % 2) * half, half), half)
        my_cols = slice(head * cols, (head + 1) * cols)
        copies = [
            pltpu.make_async_copy(q_ref.at[mine, my_cols], qbuf.at[pl.ds(0, half), :], sems.at[0]),
            pltpu.make_async_copy(q_got.at[mine, my_cols], qbuf.at[pl.ds(half, half), :], sems.at[1]),
        ]
        for copy in copies:
            copy.start()
        m_ref[...] = jnp.full(m_ref.shape, negative, jnp.float32)
        l_ref[...] = jnp.zeros(l_ref.shape, jnp.float32)
        acc_ref[...] = jnp.zeros(acc_ref.shape, jnp.float32)
    keep_ref[...] = jnp.zeros(keep_ref.shape, jnp.float32)

    count = jnp.int32(0)
    for t in range(tiles):
        last = base + t
        first_block = jnp.maximum(bounds[2 * t] // TILE, low)
        top_block = min(last, high - 1)
        mask_below = (bounds[2 * t + 1] + TILE - 1) // TILE

        def add(back, c, t=t, last=last, top_block=top_block, mask_below=mask_below):
            block = top_block - back
            item_t[c] = jnp.int32(t)
            item_k[c] = block
            item_m[c] = ((block == last) | (block < mask_below)).astype(jnp.int32)
            return c + 1

        count = lax.fori_loop(0, top_block - first_block + 1, add, count)
    for extra in range(2):
        item_t[count + extra] = jnp.int32(tiles)
        item_k[count + extra] = jnp.int32(low)
        item_m[count + extra] = jnp.int32(0)

    def load(ref, n):
        kbuf[pl.ds(n * rows, rows), :] = ref[pl.ds(0, rows), :]
        for i in range(tiles):
            vbuf[n * tiles + i] = ref[pl.ds(rows + i * TILE, TILE), :].T

    def load_all():
        for n, ref in enumerate(messages):
            if n == 0 and far is not None:
                stretch = stretch_of(me, cp_size)
                is_far = functools.reduce(jnp.logical_or, [stretch == s for s in far_stretches])

                @pl.when(is_far)
                def from_far():
                    load(far, 0)

                @pl.when(jnp.logical_not(is_far))
                def from_near(ref=ref):
                    load(ref, 0)
            else:
                load(ref, n)

    def body(i, carry):
        t1, k1, t2, k2 = carry
        t = item_t[i]
        block = item_k[i]
        masked = item_m[i]

        @pl.when(masked == 1)
        def make_bias():
            key_pos = block * TILE + lax.broadcasted_iota(jnp.int32, (TILE, TILE), 0)
            own = (base + t) * TILE + lax.broadcasted_iota(jnp.int32, (TILE, TILE), 1)
            allowed = (key_pos >= starts[t]) & (key_pos <= own)
            bias_ref[...] = jnp.where(allowed, 0.0, negative)

        q_rows = pl.ds(pl.multiple_of(jnp.minimum(t, tiles - 1) * TILE, TILE), TILE)
        k_rows = pl.ds(pl.multiple_of((block - low) * TILE, TILE), TILE)

        def stages(with_mask):
            for h in range(group):
                slot = t2 * group + h
                acc_ref[slot] = keep_ref[0, h] * acc_ref[slot] + jnp.dot(
                    vbuf[k2 - low], p_ref[h], preferred_element_type=jnp.float32
                )
            for h in range(group):
                slot = t1 * group + h
                keep = keep_ref[1, h]
                keep_ref[0, h] = keep
                weights = jnp.exp2((s_ref[h] - m_ref[slot]) * factor)
                l_ref[slot] = keep * l_ref[slot] + jnp.sum(weights, axis=0, keepdims=True)
                p_ref[h] = weights.astype(jnp.bfloat16)
            for h in range(group):
                slot = t * group + h
                scores = lax.dot_general(
                    kbuf[k_rows, :], qbuf[q_rows, h * HEAD : (h + 1) * HEAD],
                    (((1,), (1,)), ((), ())), preferred_element_type=jnp.float32,
                )
                if with_mask:
                    scores = scores + bias_ref[...]
                s_ref[h] = scores
                old = m_ref[slot]
                new = jnp.maximum(old, jnp.max(scores, axis=0, keepdims=True))
                m_ref[slot] = new
                keep_ref[1, h] = jnp.exp2((old - new) * factor)

        @pl.when(masked == 1)
        def with_mask():
            stages(True)

        @pl.when(masked == 0)
        def without_mask():
            stages(False)

        return (t, block, t1, k1)

    def run():
        load_all()
        start = (jnp.int32(tiles), jnp.int32(low)) * 2
        lax.fori_loop(0, count + 2, body, start)

    if opening:
        for copy in copies:
            copy.wait()
        run()
    else:
        pl.when(count > 0)(run)

    if closing:
        for t in range(tiles):
            for h in range(group):
                slot = t * group + h
                obuf[pl.ds(t * TILE, TILE), h * HEAD : (h + 1) * HEAD] = (
                    (acc_ref[slot] / l_ref[slot]).astype(obuf.dtype).T
                )
        size = rows // pieces
        run_all([
            pltpu.make_async_copy(
                obuf.at[pl.ds(pl.multiple_of(((my_tp + k) % pieces) * size, size), size), :],
                outs[k], sems.at[k],
            )
            for k in range(pieces)
        ])


def attend(head, low, group, pieces, cp_size, far_stretches, bounds, starts, q_pair, messages, state=None, closing=True):
    opening = state is None
    rows = messages[0].shape[0] // 2
    cols = group * HEAD
    tiles = rows // TILE
    stretches = len(messages) - (low == 0)
    high = low + stretches * tiles
    slots = (tiles + 1) * group
    held = [
        ((rows, cols), jnp.bfloat16),
        ((slots, 1, TILE), jnp.float32),
        ((slots, 1, TILE), jnp.float32),
        ((slots, HEAD, TILE), jnp.float32),
    ]
    scratch = [
        pltpu.VMEM((stretches * rows, HEAD), jnp.bfloat16),
        pltpu.VMEM((stretches * tiles, HEAD, TILE), jnp.bfloat16),
        pltpu.VMEM((2, group, 1, TILE), jnp.float32),
        pltpu.VMEM((group, TILE, TILE), jnp.float32),
        pltpu.VMEM((group, TILE, TILE), jnp.bfloat16),
        pltpu.VMEM((TILE, TILE), jnp.float32),
        pltpu.SMEM((40,), jnp.int32),
        pltpu.SMEM((40,), jnp.int32),
        pltpu.SMEM((40,), jnp.int32),
    ]
    outs = []
    if closing:
        scratch.append(pltpu.VMEM((rows, cols), jnp.bfloat16))
        outs = [jax.ShapeDtypeStruct((rows // pieces, cols), jnp.bfloat16)] * pieces
    scratch.append(pltpu.SemaphoreType.DMA((8,)))
    operands = [bounds, starts]
    specs = [scalars, fast]
    if opening:
        operands += list(q_pair)
        specs += [anywhere, fast]
    operands += messages
    specs += [fast] * len(messages)
    aliases = {}
    if opening and closing:
        scratch = [pltpu.VMEM(*h) for h in held] + scratch
    else:
        if not opening:
            for n in range(len(held)):
                aliases[len(operands) + n] = len(outs) + n
            operands += state
            specs += [fast] * len(held)
        outs = outs + [jax.ShapeDtypeStruct(*h) for h in held]
    return pl.pallas_call(
        functools.partial(
            attend_kernel, head, low, high, opening, closing, pieces, cp_size, far_stretches
        ),
        in_specs=specs,
        out_specs=[fast] * len(outs),
        out_shape=outs,
        scratch_shapes=scratch,
        input_output_aliases=aliases,
        compiler_params=pltpu.CompilerParams(vmem_limit_bytes=12 << 20),
    )(*operands)


def stretch_of(device, cp_size):
    return jnp.where(device % 2 == 0, device // 2, cp_size - 1 - device // 2)


def docs_kernel(rows, cp_size, lengths, bounds_ref, starts_ref):
    stretch = stretch_of(lax.axis_index("cp"), cp_size)
    origin = (stretch - 2) * rows
    tiles = rows // TILE
    pos = [
        2 * rows + t * TILE + lax.broadcasted_iota(jnp.int32, (8, TILE), 1) for t in range(tiles)
    ]

    def step(j, carry):
        end, edges, begins = carry
        end = end + lengths[j]
        edges = tuple(
            jnp.where(end <= 2 * rows + (n // 2) * TILE + (n % 2) * (TILE - 1), end, e)
            for n, e in enumerate(edges)
        )
        begins = tuple(jnp.where(p >= end, end, b) for p, b in zip(pos, begins))
        return end, edges, begins

    start = -origin
    edges = (start,) * (2 * tiles)
    begins = tuple(jnp.full((8, TILE), start, jnp.int32) for _ in range(tiles))
    _, edges, begins = lax.fori_loop(0, lengths.shape[0], step, (start, edges, begins))
    for n in range(2 * tiles):
        bounds_ref[n] = edges[n]
    for t in range(tiles):
        starts_ref[t] = begins[t][:1]


def docs(lengths, rows, cp_size):
    tiles = rows // TILE
    return pl.pallas_call(
        functools.partial(docs_kernel, rows, cp_size),
        in_specs=[scalars],
        out_specs=[scalars, fast],
        out_shape=[
            jax.ShapeDtypeStruct((2 * tiles,), jnp.int32),
            jax.ShapeDtypeStruct((tiles, 1, TILE), jnp.int32),
        ],
        compiler_params=pltpu.CompilerParams(vmem_limit_bytes=1 << 20),
    )(lengths)


def place_kernel(head, heads, *refs):
    pieces = len(refs) - 2 - (head > 0)
    out, sems = refs[-2:]
    _, cols = refs[0].shape
    t = lax.axis_index("tp")
    j = t % 2 + 2 * jnp.where(lax.axis_index("cp") % 2 == t // 2, 0, 1)
    run_all([
        pltpu.make_async_copy(
            refs[k],
            out.at[:, pl.ds(pl.multiple_of(((j + pieces - k) % pieces) * (heads * cols) + head * cols, cols), cols)],
            sems.at[k],
        )
        for k in range(pieces)
    ])


def place(head, heads, pieces, result):
    rows, cols = pieces[0].shape
    operands = [*pieces] + ([] if result is None else [result])
    return pl.pallas_call(
        functools.partial(place_kernel, head, heads),
        in_specs=[fast] * len(pieces) + [anywhere] * (result is not None),
        out_specs=anywhere,
        out_shape=jax.ShapeDtypeStruct((rows, cols * heads * len(pieces)), pieces[0].dtype),
        scratch_shapes=[pltpu.SemaphoreType.DMA((len(pieces),))],
        input_output_aliases={} if result is None else {len(operands) - 1: 0},
        compiler_params=pltpu.CompilerParams(vmem_limit_bytes=4 << 20),
    )(*operands)


def on_device(queries, keys, values, doc_lengths):
    tok_rows, q_cols = queries.shape
    kv_local = keys.shape[1] // HEAD
    group_cols = q_cols // kv_local
    cp_size = lax.axis_size("cp")
    tp_size = lax.axis_size("tp")

    swap = [(i, i ^ 1) for i in range(cp_size)]
    link = lambda s, d: (device_of(s, cp_size), device_of(s + d, cp_size))
    ahead = [link(s, 1) for s in range(cp_size - 1)]
    long_hops = [cp_size // 4 - 1, cp_size - 1 - cp_size // 4]
    handed = [link(s, 1) for s in range(cp_size - 1) if s not in long_hops]
    direct = [link(s - 1, 2) for s in long_hops]
    far_stretches = [s + 1 for s in long_hops]

    def route(k):
        pairs = []
        for c in range(cp_size):
            for t in range(tp_size):
                j = (t + k) % tp_size
                dest_c = c if j < 2 else c ^ 1
                dest_t = j % 2 + 2 * (c % 2)
                pairs.append((c * tp_size + t, dest_c * tp_size + dest_t))
        return pairs

    k_got = lax.ppermute(keys, "cp", swap)
    v_got = lax.ppermute(values, "cp", swap)
    q_got = lax.ppermute(queries, "cp", swap)
    bounds, starts = docs(doc_lengths, tok_rows, cp_size)
    messages = join(bounds, keys, values, k_got, v_got)

    near = [lax.ppermute(messages[h], "cp", ahead) for h in range(kv_local)]
    far = [lax.ppermute(messages[h], "cp", direct) for h in range(kv_local)]
    next_near = [lax.ppermute(near[h], "cp", handed) for h in range(kv_local)]
    group = group_cols // HEAD
    tiles = tok_rows // TILE
    q_pair = (queries, q_got)
    received = []
    for h in range(kv_local):
        if h == 0:
            state = attend(h, tiles, group, tp_size, cp_size, far_stretches, bounds, starts, q_pair,
                          [near[h], messages[h]], closing=False)
            out = attend(h, 0, group, tp_size, cp_size, far_stretches, bounds, starts, q_pair,
                        [far[h], next_near[h]], state=state)
        else:
            out = attend(h, 0, group, tp_size, cp_size, far_stretches, bounds, starts, q_pair,
                        [far[h], next_near[h], near[h], messages[h]])
        received.append([lax.ppermute(out[k], ("cp", "tp"), route(k)) for k in range(tp_size)])

    result = None
    for h in range(kv_local):
        result = place(h, kv_local, received[h], result)
    return result


def solution(mesh):
    in_specs = (P("cp", "tp"), P("cp", "tp"), P("cp", "tp"), P())
    out_specs = P(("cp", "tp"), None)
    return jax.shard_map(on_device, mesh=mesh, in_specs=in_specs, out_specs=out_specs, check_vma=False)
```

profile of v0, /device:TPU:162, one launch (start us, length us, event | category | flops | bytes accessed | tf_op | source)
XLA Modules:
  0.0 113.5 jit_solution(16429125482287021453)
XLA Ops:
  0.0 0.0 collective-permute-start
  0.0 0.5 collective-permute-start.1
  0.5 0.0 collective-permute-start.2
  0.5 0.0 copy-start.4
  0.5 0.7 copy-done.4
  1.2 2.0 %shard_map.46 = (s32[6]{0:T(128)S(1)}, s32[3,1,256]{2,1,0:T(1,128)S(1)}) custom-call(s32[64]{0:T(128)S(1)} %copy-done.4), custom_call_target="tpu_custom_call" | custom-call | tf_op jit(solution)/shard_map/pallas_call | solution.py:317
  3.2 1.5 %collective-permute-done.1.k_got = bf16[768,256]{1,0:T(8,128)(2,1)S(1)} collective-permute-done((bf16[768,256]{1,0:T(8,128)(2,1)}, bf16[768,256]{1,0:T(8,128)(2,1)S(1)}, u32[]{:S(2)}, u32[]{:S(2)}) %collective-permute-start.1) | collective-permute-done | bytes 393248 | tf_op jit(solution)/shard_map/ppermute | solution.py:384
  4.7 0.6 collective-permute-done.2.v_got
  5.3 1.0 copy-done.2
  6.3 1.0 copy-done.3
  7.3 0.8 shard_map.47
  8.1 3.4 %collective-permute-start.11 = (bf16[1536,128]{1,0:T(8,128)(2,1)S(1)}, bf16[1536,128]{1,0:T(8,128)(2,1)S(1)}, u32[]{:S(2)}, u32[]{:S(2)}) collective-permute-start(bf16[1536,128]{1,0:T(8,128)(2,1)S(1)} %get-tuple-element.28.refs_5_), channel_id=1, source_target_pairs={{0,8},{8,16},{16,24},{24,32},{32,40},{40,48},{48,56},{56,64},{64,7... | collective-permute-start | bytes 1179656 | tf_op jit(solution)/shard_map/ppermute | solution.py:390
  11.5 3.1 %collective-permute-start.4 = (bf16[1536,128]{1,0:T(8,128)(2,1)S(1)}, bf16[1536,128]{1,0:T(8,128)(2,1)S(1)}, u32[]{:S(2)}, u32[]{:S(2)}) collective-permute-start(bf16[1536,128]{1,0:T(8,128)(2,1)S(1)} %get-tuple-element.23.refs_7_), channel_id=1, source_target_pairs={{0,8},{8,16},{16,24},{24,32},{32,40},{40,48},{48,56},{56,64},{64,7... | collective-permute-start | bytes 1179656 | tf_op jit(solution)/shard_map/ppermute | solution.py:390
  14.6 0.7 collective-permute-start.10
  15.3 2.5 %collective-permute-done.11.refs_4_ = bf16[1536,128]{1,0:T(8,128)(2,1)S(1)} collective-permute-done((bf16[1536,128]{1,0:T(8,128)(2,1)S(1)}, bf16[1536,128]{1,0:T(8,128)(2,1)S(1)}, u32[]{:S(2)}, u32[]{:S(2)}) %collective-permute-start.11) | collective-permute-done | bytes 393248 | tf_op jit(solution)/shard_map/ppermute | solution.py:390
  17.8 3.4 %collective-permute-start.12 = (bf16[1536,128]{1,0:T(8,128)(2,1)S(1)}, bf16[1536,128]{1,0:T(8,128)(2,1)S(1)}, u32[]{:S(2)}, u32[]{:S(2)}) collective-permute-start(bf16[1536,128]{1,0:T(8,128)(2,1)S(1)} %collective-permute-done.11.refs_4_), channel_id=1, source_target_pairs={{0,8},{8,16},{16,24},{24,32},{32,40},{40,48},{48,56},{56,64},{64,7... | collective-permute-start | bytes 1179656 | tf_op jit(solution)/shard_map/ppermute | solution.py:392
  21.2 0.7 collective-permute-start.3
  21.9 0.1 collective-permute-done.4.refs_6_
  22.0 3.4 %collective-permute-start.5 = (bf16[1536,128]{1,0:T(8,128)(2,1)S(1)}, bf16[1536,128]{1,0:T(8,128)(2,1)S(1)}, u32[]{:S(2)}, u32[]{:S(2)}) collective-permute-start(bf16[1536,128]{1,0:T(8,128)(2,1)S(1)} %collective-permute-done.4.refs_6_), channel_id=1, source_target_pairs={{0,8},{8,16},{16,24},{24,32},{32,40},{40,48},{48,56},{56,64},{64,7... | collective-permute-start | bytes 1179656 | tf_op jit(solution)/shard_map/ppermute | solution.py:392
  25.4 0.0 collective-permute-done.refs_3_
  25.4 0.0 copy-start
  25.4 1.5 %copy-done = bf16[768,1280]{1,0:T(8,128)(2,1)S(1)} copy-done((bf16[768,1280]{1,0:T(8,128)(2,1)S(1)}, bf16[768,1280]{1,0:T(8,128)(2,1)}, u32[]{:S(2)}) %copy-start) | copy-done | bytes 1966104
  26.9 6.5 %shard_map.49 = (bf16[768,640]{1,0:T(8,128)(2,1)S(1)}, f32[20,1,256]{2,1,0:T(1,128)S(1)}, f32[20,1,256]{2,1,0:T(1,128)S(1)}, f32[20,128,256]{2,1,0:T(8,128)S(1)}) custom-call(s32[6]{0:T(128)S(1)} %get-tuple-element.21.bounds.refs_0_, s32[3,1,256]{2,1,0:T(1,128)S(1)} %get-tuple-element.22.refs_1_, bf16[768,1280]{1,0:T(8,128)(2,1)S(1)} %copy-done, ...), custom_call_target="tpu_custom_call" | custom-call | tf_op jit(solution)/shard_map/pallas_call | solution.py:270
  33.5 0.0 collective-permute-done.10.refs_2_
  33.5 8.4 %collective-permute-done.12.refs_3_ = bf16[1536,128]{1,0:T(8,128)(2,1)S(1)} collective-permute-done((bf16[1536,128]{1,0:T(8,128)(2,1)S(1)}, bf16[1536,128]{1,0:T(8,128)(2,1)S(1)}, u32[]{:S(2)}, u32[]{:S(2)}) %collective-permute-start.12) | collective-permute-done | bytes 393248 | tf_op jit(solution)/shard_map/ppermute | solution.py:392
  41.9 2.3 %shard_map.50 = (bf16[192,640]{1,0:T(8,128)(2,1)S(1)}, bf16[192,640]{1,0:T(8,128)(2,1)S(1)}, bf16[192,640]{1,0:T(8,128)(2,1)S(1)}, bf16[192,640]{1,0:T(8,128)(2,...) custom-call(s32[6]{0:T(128)S(1)} %get-tuple-element.21.bounds.refs_0, ...), custom_call_target="tpu_custom_call", output_to_operand_aliasing={{4}: (4, {}), {5}: (5, {}), {6}: (6, {}), {7}: (7, {})} | custom-call | tf_op jit(solution)/shard_map/pallas_call | solution.py:270
  44.1 0.7 collective-permute-start.13
  44.8 22.0 %collective-permute-start.14 = (bf16[192,640]{1,0:T(8,128)(2,1)S(1)}, bf16[192,640]{1,0:T(8,128)(2,1)S(1)}, u32[]{:S(2)}, u32[]{:S(2)}) collective-permute-start(bf16[192,640]{1,0:T(8,128)(2,1)S(1)} %get-tuple-element.34), channel_id=1, source_target_pairs={{0,1},{1,4},{2,5},{3,0},{4,7},{5,2},{6,3},{7,6},{8,9},{9,12},{10,1... | collective-permute-start | bytes 737288 | tf_op jit(solution)/shard_map/ppermute | solution.py:406
  66.8 1.9 %collective-permute-start.15 = (bf16[192,640]{1,0:T(8,128)(2,1)S(1)}, bf16[192,640]{1,0:T(8,128)(2,1)S(1)}, u32[]{:S(2)}, u32[]{:S(2)}) collective-permute-start(bf16[192,640]{1,0:T(8,128)(2,1)S(1)} %get-tuple-element.35), channel_id=1, source_target_pairs={{0,4},{1,5},{2,0},{3,1},{4,2},{5,3},{6,6},{7,7},{8,12},{9,13},{10,... | collective-permute-start | bytes 737288 | tf_op jit(solution)/shard_map/ppermute | solution.py:406
  68.7 0.0 collective-permute-done.3.refs_4_
  68.7 0.0 collective-permute-done.5.refs_5_
  68.7 0.0 copy-done.1
  68.8 8.4 %shard_map.48 = (bf16[192,640]{1,0:T(8,128)(2,1)S(1)}, bf16[192,640]{1,0:T(8,128)(2,1)S(1)}, bf16[192,640]{1,0:T(8,128)(2,1)S(1)}, bf16[192,640]{1,0:T(8,128)(2,1)S(1)}) custom-call(s32[6]{0:T(128)S(1)} %get-tuple-element.21.bounds.refs_0_, s32[3,1,256]{2,1,0:T(1,128)S(1)} %get-tuple-element.22.refs_1_, bf16[768,1280]{1,0:T(8,128)(2,1)S(1)} %copy-done.1, ...), custom_call_target="tpu_custom_call" | custom-call | tf_op jit(solution)/shard_map/pallas_call | solution.py:270
  77.2 0.7 collective-permute-start.6
  77.8 6.3 %collective-permute-start.7 = (bf16[192,640]{1,0:T(8,128)(2,1)S(1)}, bf16[192,640]{1,0:T(8,128)(2,1)S(1)}, u32[]{:S(2)}, u32[]{:S(2)}) collective-permute-start(bf16[192,640]{1,0:T(8,128)(2,1)S(1)} %get-tuple-element.25), channel_id=1, source_target_pairs={{0,1},{1,4},{2,5},{3,0},{4,7},{5,2},{6,3},{7,6},{8,9},{9,12},{10,1... | collective-permute-start | bytes 737288 | tf_op jit(solution)/shard_map/ppermute | solution.py:406
  84.2 0.0 collective-permute-done.13.refs_0_
  84.2 0.0 collective-permute-start.16
  84.2 0.0 collective-permute-done.14.refs_1_
  84.2 3.5 %collective-permute-start.8 = (bf16[192,640]{1,0:T(8,128)(2,1)S(1)}, bf16[192,640]{1,0:T(8,128)(2,1)S(1)}, u32[]{:S(2)}, u32[]{:S(2)}) collective-permute-start(bf16[192,640]{1,0:T(8,128)(2,1)S(1)} %get-tuple-element.26), channel_id=1, source_target_pairs={{0,4},{1,5},{2,0},{3,1},{4,2},{5,3},{6,6},{7,7},{8,12},{9,13},{10,... | collective-permute-start | bytes 737288 | tf_op jit(solution)/shard_map/ppermute | solution.py:406
  87.6 0.0 collective-permute-done.15.refs_2_
  87.7 1.7 %collective-permute-start.9 = (bf16[192,640]{1,0:T(8,128)(2,1)S(1)}, bf16[192,640]{1,0:T(8,128)(2,1)S(1)}, u32[]{:S(2)}, u32[]{:S(2)}) collective-permute-start(bf16[192,640]{1,0:T(8,128)(2,1)S(1)} %get-tuple-element.27), channel_id=1, source_target_pairs={{0,5},{1,0},{2,1},{3,4},{4,3},{5,6},{6,7},{7,2},{8,13},{9,8},{10,9... | collective-permute-start | bytes 737288 | tf_op jit(solution)/shard_map/ppermute | solution.py:406
  89.4 17.9 %collective-permute-done.16.refs_3_ = bf16[192,640]{1,0:T(8,128)(2,1)S(1)} collective-permute-done((bf16[192,640]{1,0:T(8,128)(2,1)S(1)}, bf16[192,640]{1,0:T(8,128)(2,1)S(1)}, u32[]{:S(2)}, u32[]{:S(2)}) %collective-permute-start.16) | collective-permute-done | bytes 245792 | tf_op jit(solution)/shard_map/ppermute | solution.py:406
  107.3 1.0 shard_map.51.refs_4_
  108.2 0.0 collective-permute-done.6.refs_0_
  108.2 0.0 collective-permute-done.7.refs_1_
  108.2 0.0 collective-permute-done.8.refs_2_
  108.3 4.3 %collective-permute-done.9.refs_3_ = bf16[192,640]{1,0:T(8,128)(2,1)S(1)} collective-permute-done((bf16[192,640]{1,0:T(8,128)(2,1)S(1)}, bf16[192,640]{1,0:T(8,128)(2,1)S(1)}, u32[]{:S(2)}, u32[]{:S(2)}) %collective-permute-start.9) | collective-permute-done | bytes 245792 | tf_op jit(solution)/shard_map/ppermute | solution.py:406
  112.5 1.0 shard_map.52
  (3 shorter events, 0.0 us)
Async XLA Ops:
  0.0 25.4 %collective-permute-start = (bf16[768,1280]{1,0:T(8,128)(2,1)}, bf16[768,1280]{1,0:T(8,128)(2,1)S(1)}, u32[]{:S(2)}, u32[]{:S(2)}) collective-permute-start(bf16[768,1280]{1,0:T(8,128)(2,1)} %refs_2_.3), channel_id=1, source_target_pairs={{0,4},{4,0},{8,12},{12,8},{16,20},{20,16},{24,28},{28,24},{32,36},... | collective-permute-start | bytes 5898248 | tf_op jit(solution)/shard_map/ppermute | solution.py:386
  0.0 4.7 %collective-permute-start.1 = (bf16[768,256]{1,0:T(8,128)(2,1)}, bf16[768,256]{1,0:T(8,128)(2,1)S(1)}, u32[]{:S(2)}, u32[]{:S(2)}) collective-permute-start(bf16[768,256]{1,0:T(8,128)(2,1)} %k_ref.1), channel_id=1, source_target_pairs={{0,4},{4,0},{8,12},{12,8},{16,20},{20,16},{24,28},{28,24},{32,36},... | collective-permute-start | bytes 1179656 | tf_op jit(solution)/shard_map/ppermute | solution.py:384
  0.5 4.8 %collective-permute-start.2 = (bf16[768,256]{1,0:T(8,128)(2,1)}, bf16[768,256]{1,0:T(8,128)(2,1)S(1)}, u32[]{:S(2)}, u32[]{:S(2)}) collective-permute-start(bf16[768,256]{1,0:T(8,128)(2,1)} %v_ref.1), channel_id=1, source_target_pairs={{0,4},{4,0},{8,12},{12,8},{16,20},{20,16},{24,28},{28,24},{32,36},... | collective-permute-start | bytes 1179656 | tf_op jit(solution)/shard_map/ppermute | solution.py:385
  0.5 0.7 copy-start.4
  5.3 1.0 copy-start.2
  6.3 1.0 copy-start.3
  8.1 9.7 %collective-permute-start.11 = (bf16[1536,128]{1,0:T(8,128)(2,1)S(1)}, bf16[1536,128]{1,0:T(8,128)(2,1)S(1)}, u32[]{:S(2)}, u32[]{:S(2)}) collective-permute-start(bf16[1536,128]{1,0:T(8,128)(2,1)S(1)} %get-tuple-element.28.refs_5_), channel_id=1, source_target_pairs={{0,8},{8,16},{16,24},{24,32},{32,40},{40,48},{48,56},{56,64},{64,7... | collective-permute-start | bytes 1179656 | tf_op jit(solution)/shard_map/ppermute | solution.py:390
  11.5 10.5 %collective-permute-start.4 = (bf16[1536,128]{1,0:T(8,128)(2,1)S(1)}, bf16[1536,128]{1,0:T(8,128)(2,1)S(1)}, u32[]{:S(2)}, u32[]{:S(2)}) collective-permute-start(bf16[1536,128]{1,0:T(8,128)(2,1)S(1)} %get-tuple-element.23.refs_7_), channel_id=1, source_target_pairs={{0,8},{8,16},{16,24},{24,32},{32,40},{40,48},{48,56},{56,64},{64,7... | collective-permute-start | bytes 1179656 | tf_op jit(solution)/shard_map/ppermute | solution.py:390
  14.6 18.8 %collective-permute-start.10 = (bf16[1536,128]{1,0:T(8,128)(2,1)S(1)}, bf16[1536,128]{1,0:T(8,128)(2,1)S(1)}, u32[]{:S(2)}, u32[]{:S(2)}) collective-permute-start(bf16[1536,128]{1,0:T(8,128)(2,1)S(1)} %get-tuple-element.28.refs_5_), channel_id=1, source_target_pairs={{112,128},{140,124},{113,129},{141,125},{114,130},{142,126},{115,1... | collective-permute-start | bytes 1179656 | tf_op jit(solution)/shard_map/ppermute | solution.py:391
  17.8 24.1 %collective-permute-start.12 = (bf16[1536,128]{1,0:T(8,128)(2,1)S(1)}, bf16[1536,128]{1,0:T(8,128)(2,1)S(1)}, u32[]{:S(2)}, u32[]{:S(2)}) collective-permute-start(bf16[1536,128]{1,0:T(8,128)(2,1)S(1)} %collective-permute-done.11.refs_4_), channel_id=1, source_target_pairs={{0,8},{8,16},{16,24},{24,32},{32,40},{40,48},{48,56},{56,64},{64,7... | collective-permute-start | bytes 1179656 | tf_op jit(solution)/shard_map/ppermute | solution.py:392
  21.2 47.6 %collective-permute-start.3 = (bf16[1536,128]{1,0:T(8,128)(2,1)S(1)}, bf16[1536,128]{1,0:T(8,128)(2,1)S(1)}, u32[]{:S(2)}, u32[]{:S(2)}) collective-permute-start(bf16[1536,128]{1,0:T(8,128)(2,1)S(1)} %get-tuple-element.23.refs_7_), channel_id=1, source_target_pairs={{112,128},{140,124},{113,129},{141,125},{114,130},{142,126},{115,1... | collective-permute-start | bytes 1179656 | tf_op jit(solution)/shard_map/ppermute | solution.py:391
  22.0 46.8 %collective-permute-start.5 = (bf16[1536,128]{1,0:T(8,128)(2,1)S(1)}, bf16[1536,128]{1,0:T(8,128)(2,1)S(1)}, u32[]{:S(2)}, u32[]{:S(2)}) collective-permute-start(bf16[1536,128]{1,0:T(8,128)(2,1)S(1)} %collective-permute-done.4.refs_6_), channel_id=1, source_target_pairs={{0,8},{8,16},{16,24},{24,32},{32,40},{40,48},{48,56},{56,64},{64,7... | collective-permute-start | bytes 1179656 | tf_op jit(solution)/shard_map/ppermute | solution.py:392
  25.4 1.5 %copy-start = (bf16[768,1280]{1,0:T(8,128)(2,1)S(1)}, bf16[768,1280]{1,0:T(8,128)(2,1)}, u32[]{:S(2)}) copy-start(bf16[768,1280]{1,0:T(8,128)(2,1)} %refs_2_.3) | copy-start | bytes 5898244
  41.9 26.9 %copy-start.1 = (bf16[768,1280]{1,0:T(8,128)(2,1)S(1)}, bf16[768,1280]{1,0:T(8,128)(2,1)}, u32[]{:S(2)}) copy-start(bf16[768,1280]{1,0:T(8,128)(2,1)} %refs_2_.3) | copy-start | bytes 5898244
  44.1 40.0 %collective-permute-start.13 = (bf16[192,640]{1,0:T(8,128)(2,1)S(1)}, bf16[192,640]{1,0:T(8,128)(2,1)S(1)}, u32[]{:S(2)}, u32[]{:S(2)}) collective-permute-start(bf16[192,640]{1,0:T(8,128)(2,1)S(1)} %get-tuple-element.33), channel_id=1, source_target_pairs={{0,0},{1,1},{2,4},{3,5},{4,6},{5,7},{6,2},{7,3},{8,8},{9,9},{10,12... | collective-permute-start | bytes 737288 | tf_op jit(solution)/shard_map/ppermute | solution.py:406
  44.8 39.3 %collective-permute-start.14 = (bf16[192,640]{1,0:T(8,128)(2,1)S(1)}, bf16[192,640]{1,0:T(8,128)(2,1)S(1)}, u32[]{:S(2)}, u32[]{:S(2)}) collective-permute-start(bf16[192,640]{1,0:T(8,128)(2,1)S(1)} %get-tuple-element.34), channel_id=1, source_target_pairs={{0,1},{1,4},{2,5},{3,0},{4,7},{5,2},{6,3},{7,6},{8,9},{9,12},{10,1... | collective-permute-start | bytes 737288 | tf_op jit(solution)/shard_map/ppermute | solution.py:406
  66.8 20.8 %collective-permute-start.15 = (bf16[192,640]{1,0:T(8,128)(2,1)S(1)}, bf16[192,640]{1,0:T(8,128)(2,1)S(1)}, u32[]{:S(2)}, u32[]{:S(2)}) collective-permute-start(bf16[192,640]{1,0:T(8,128)(2,1)S(1)} %get-tuple-element.35), channel_id=1, source_target_pairs={{0,4},{1,5},{2,0},{3,1},{4,2},{5,3},{6,6},{7,7},{8,12},{9,13},{10,... | collective-permute-start | bytes 737288 | tf_op jit(solution)/shard_map/ppermute | solution.py:406
  77.2 31.1 %collective-permute-start.6 = (bf16[192,640]{1,0:T(8,128)(2,1)S(1)}, bf16[192,640]{1,0:T(8,128)(2,1)S(1)}, u32[]{:S(2)}, u32[]{:S(2)}) collective-permute-start(bf16[192,640]{1,0:T(8,128)(2,1)S(1)} %get-tuple-element.24), channel_id=1, source_target_pairs={{0,0},{1,1},{2,4},{3,5},{4,6},{5,7},{6,2},{7,3},{8,8},{9,9},{10,12... | collective-permute-start | bytes 737288 | tf_op jit(solution)/shard_map/ppermute | solution.py:406
  77.8 30.4 %collective-permute-start.7 = (bf16[192,640]{1,0:T(8,128)(2,1)S(1)}, bf16[192,640]{1,0:T(8,128)(2,1)S(1)}, u32[]{:S(2)}, u32[]{:S(2)}) collective-permute-start(bf16[192,640]{1,0:T(8,128)(2,1)S(1)} %get-tuple-element.25), channel_id=1, source_target_pairs={{0,1},{1,4},{2,5},{3,0},{4,7},{5,2},{6,3},{7,6},{8,9},{9,12},{10,1... | collective-permute-start | bytes 737288 | tf_op jit(solution)/shard_map/ppermute | solution.py:406
  84.2 23.1 %collective-permute-start.16 = (bf16[192,640]{1,0:T(8,128)(2,1)S(1)}, bf16[192,640]{1,0:T(8,128)(2,1)S(1)}, u32[]{:S(2)}, u32[]{:S(2)}) collective-permute-start(bf16[192,640]{1,0:T(8,128)(2,1)S(1)} %get-tuple-element.36), channel_id=1, source_target_pairs={{0,5},{1,0},{2,1},{3,4},{4,3},{5,6},{6,7},{7,2},{8,13},{9,8},{10,9... | collective-permute-start | bytes 737288 | tf_op jit(solution)/shard_map/ppermute | solution.py:406
  84.2 24.1 %collective-permute-start.8 = (bf16[192,640]{1,0:T(8,128)(2,1)S(1)}, bf16[192,640]{1,0:T(8,128)(2,1)S(1)}, u32[]{:S(2)}, u32[]{:S(2)}) collective-permute-start(bf16[192,640]{1,0:T(8,128)(2,1)S(1)} %get-tuple-element.26), channel_id=1, source_target_pairs={{0,4},{1,5},{2,0},{3,1},{4,2},{5,3},{6,6},{7,7},{8,12},{9,13},{10,... | collective-permute-start | bytes 737288 | tf_op jit(solution)/shard_map/ppermute | solution.py:406
  87.7 24.9 %collective-permute-start.9 = (bf16[192,640]{1,0:T(8,128)(2,1)S(1)}, bf16[192,640]{1,0:T(8,128)(2,1)S(1)}, u32[]{:S(2)}, u32[]{:S(2)}) collective-permute-start(bf16[192,640]{1,0:T(8,128)(2,1)S(1)} %get-tuple-element.27), channel_id=1, source_target_pairs={{0,5},{1,0},{2,1},{3,4},{4,3},{5,6},{6,7},{7,2},{8,13},{9,8},{10,9... | collective-permute-start | bytes 737288 | tf_op jit(solution)/shard_map/ppermute | solution.py:406
where the time goes:
time: 114 us; the launch traced here: 113 us
  starting transfers between devices  51.9 us (46%)
  waiting for transfers between devices  35.3 us (31%)
  Pallas kernels  21.9 us (19%)
  local copies, waits for them, and re-layouts  4.19 us (4%)
    ppermute x8, starting transfers between devices, on_device(): lax.ppermute(out[k], ('cp', 'tp'), route(k))  36.7 us
    ppermute x8, waiting for transfers between devices, on_device(): lax.ppermute(out[k], ('cp', 'tp'), route(k))  22.2 us
    pallas_call x3, Pallas kernels, attend(): pl.pallas_call(functools.partial(attend_kernel, head, low, high, opening,...  17.2 us
    ppermute x2, waiting for transfers between devices, on_device(): next_near = [lax.ppermute(near[h], 'cp', handed) for h in range(kv_local)]  8.4 us
    ppermute x2, starting transfers between devices, on_device(): next_near = [lax.ppermute(near[h], 'cp', handed) for h in range(kv_local)]  6.78 us
    ppermute x2, starting transfers between devices, on_device(): near = [lax.ppermute(messages[h], 'cp', ahead) for h in range(kv_local)]  6.51 us
    unnamed x10, local copies, waits for them, and re-layouts  4.19 us
    ppermute x2, waiting for transfers between devices, on_device(): near = [lax.ppermute(messages[h], 'cp', ahead) for h in range(kv_local)]  2.58 us
  transfers between devices with their start and end apart: 17, of which 7 were waited for; matrix products, arithmetic and copies ran while one was open for 0% of the time, Pallas kernels for 18%

commit v1 on v0

--- a/solution.py
+++ b/solution.py
@@ -32,31 +32,32 @@
         copy.wait()
 
 
-def join_kernel(half, heads, bounds, k_ref, v_ref, k_got, v_got, *rest):
-    del bounds
-    outs, sems = rest[:heads], rest[heads]
+def join_kernel(half, heads, k_ref, v_ref, k_got, v_got, *rest):
+    outs, every, sems = rest[:heads], rest[heads], rest[heads + 1]
     mine = pl.ds(pl.multiple_of((lax.axis_index("cp") % 2) * half, half), half)
     copies = []
     for h in range(heads):
         cols = slice(h * HEAD, (h + 1) * HEAD)
         for n, (own, got) in enumerate(((k_ref, k_got), (v_ref, v_got))):
-            first = 2 * half * n
-            copies.append((own.at[mine, cols], outs[h].at[pl.ds(first, half), :]))
-            copies.append((got.at[mine, cols], outs[h].at[pl.ds(first + half, half), :]))
+            for out, skip in ((outs[h], 0), (every, 4 * half * h)):
+                first = skip + 2 * half * n
+                copies.append((own.at[mine, cols], out.at[pl.ds(first, half), :]))
+                copies.append((got.at[mine, cols], out.at[pl.ds(first + half, half), :]))
     run_all([pltpu.make_async_copy(a, b, sems.at[i]) for i, (a, b) in enumerate(copies)])
 
 
-def join(bounds, keys, values, k_got, v_got):
+def join(keys, values, k_got, v_got):
     rows, cols = keys.shape
     heads = cols // HEAD
     return pl.pallas_call(
         functools.partial(join_kernel, rows // 2, heads),
-        in_specs=[scalars, anywhere, anywhere, fast, fast],
-        out_specs=[fast] * heads,
-        out_shape=[jax.ShapeDtypeStruct((2 * rows, HEAD), keys.dtype)] * heads,
-        scratch_shapes=[pltpu.SemaphoreType.DMA((4 * heads,))],
+        in_specs=[anywhere, anywhere, fast, fast],
+        out_specs=[fast] * (heads + 1),
+        out_shape=[jax.ShapeDtypeStruct((2 * rows, HEAD), keys.dtype)] * heads
+        + [jax.ShapeDtypeStruct((2 * rows * heads, HEAD), keys.dtype)],
+        scratch_shapes=[pltpu.SemaphoreType.DMA((8 * heads,))],
         compiler_params=pltpu.CompilerParams(vmem_limit_bytes=4 << 20),
-    )(bounds, keys, values, k_got, v_got)
+    )(keys, values, k_got, v_got)
 
 
 def attend_kernel(head, low, high, opening, closing, pieces, cp_size, far_stretches, *refs):
@@ -117,10 +118,10 @@
         item_k[count + extra] = jnp.int32(low)
         item_m[count + extra] = jnp.int32(0)
 
-    def load(ref, n):
-        kbuf[pl.ds(n * rows, rows), :] = ref[pl.ds(0, rows), :]
+    def load(ref, n, skip=0):
+        kbuf[pl.ds(n * rows, rows), :] = ref[pl.ds(skip, rows), :]
         for i in range(tiles):
-            vbuf[n * tiles + i] = ref[pl.ds(rows + i * TILE, TILE), :].T
+            vbuf[n * tiles + i] = ref[pl.ds(skip + rows + i * TILE, TILE), :].T
 
     def load_all():
         for n, ref in enumerate(messages):
@@ -130,7 +131,7 @@
 
                 @pl.when(is_far)
                 def from_far():
-                    load(far, 0)
+                    load(far, 0, 2 * rows * head)
 
                 @pl.when(jnp.logical_not(is_far))
                 def from_near(ref=ref):
@@ -222,7 +223,7 @@
 
 def attend(head, low, group, pieces, cp_size, far_stretches, bounds, starts, q_pair, messages, state=None, closing=True):
     opening = state is None
-    rows = messages[0].shape[0] // 2
+    rows = messages[-1].shape[0] // 2
     cols = group * HEAD
     tiles = rows // TILE
     stretches = len(messages) - (low == 0)
@@ -385,10 +386,10 @@
     v_got = lax.ppermute(values, "cp", swap)
     q_got = lax.ppermute(queries, "cp", swap)
     bounds, starts = docs(doc_lengths, tok_rows, cp_size)
-    messages = join(bounds, keys, values, k_got, v_got)
+    *messages, every = join(keys, values, k_got, v_got)
 
     near = [lax.ppermute(messages[h], "cp", ahead) for h in range(kv_local)]
-    far = [lax.ppermute(messages[h], "cp", direct) for h in range(kv_local)]
+    far = lax.ppermute(every, "cp", direct)
     next_near = [lax.ppermute(near[h], "cp", handed) for h in range(kv_local)]
     group = group_cols // HEAD
     tiles = tok_rows // TILE
@@ -399,10 +400,10 @@
             state = attend(h, tiles, group, tp_size, cp_size, far_stretches, bounds, starts, q_pair,
                           [near[h], messages[h]], closing=False)
             out = attend(h, 0, group, tp_size, cp_size, far_stretches, bounds, starts, q_pair,
-                        [far[h], next_near[h]], state=state)
+                        [far, next_near[h]], state=state)
         else:
             out = attend(h, 0, group, tp_size, cp_size, far_stretches, bounds, starts, q_pair,
-                        [far[h], next_near[h], near[h], messages[h]])
+                        [far, next_near[h], near[h], messages[h]])
         received.append([lax.ppermute(out[k], ("cp", "tp"), route(k)) for k in range(tp_size)])
 
     result = None

time: 114 us -> 112 us (0.982)
  the two profiles are of different devices: /device:TPU:162 before, /device:TPU:160 now
where the time goes in v1:
time: 112 us; the launch traced here: 111 us
  waiting for transfers between devices  51.9 us (46%)
  Pallas kernels  32.4 us (29%)
  starting transfers between devices  22.5 us (20%)
  local copies, waits for them, and re-layouts  4.19 us (4%)
    pallas_call x3, Pallas kernels, attend(): pl.pallas_call(functools.partial(attend_kernel, head, low, high, opening,...  28 us
    ppermute x2, waiting for transfers between devices, on_device(): near = [lax.ppermute(messages[h], 'cp', ahead) for h in range(kv_local)]  24.6 us
    ppermute x8, waiting for transfers between devices, on_device(): lax.ppermute(out[k], ('cp', 'tp'), route(k))  22.5 us
    ppermute x8, starting transfers between devices, on_device(): lax.ppermute(out[k], ('cp', 'tp'), route(k))  11.8 us
    ppermute x2, starting transfers between devices, on_device(): near = [lax.ppermute(messages[h], 'cp', ahead) for h in range(kv_local)]  6.22 us
    ppermute x1, waiting for transfers between devices, on_device(): k_got = lax.ppermute(keys, 'cp', swap)  4.23 us
    unnamed x10, local copies, waits for them, and re-layouts  4.19 us
    ppermute x2, starting transfers between devices, on_device(): next_near = [lax.ppermute(near[h], 'cp', handed) for h in range(kv_local)]  2.61 us
  transfers between devices with their start and end apart: 16, of which 6 were waited for; matrix products, arithmetic and copies ran while one was open for 0% of the time, Pallas kernels for 28%

profile of v1, /device:TPU:160, one launch (start us, length us, event | category | flops | bytes accessed | tf_op | source)
XLA Modules:
  0.0 111.3 jit_solution(10212589264497916127)
XLA Ops:
  0.0 0.0 collective-permute-start
  0.0 0.5 collective-permute-start.1
  0.5 0.0 collective-permute-start.2
  0.5 4.2 %collective-permute-done.1.k_got = bf16[768,256]{1,0:T(8,128)(2,1)S(1)} collective-permute-done((bf16[768,256]{1,0:T(8,128)(2,1)}, bf16[768,256]{1,0:T(8,128)(2,1)S(1)}, u32[]{:S(2)}, u32[]{:S(2)}) %collective-permute-start.1) | collective-permute-done | bytes 393248 | tf_op jit(solution)/shard_map/ppermute | solution.py:385
  4.7 0.6 collective-permute-done.2.v_got
  5.3 0.0 copy-start.2
  5.3 1.0 copy-done.2
  6.3 1.0 copy-done.3
  7.3 0.4 shard_map.47
  7.8 3.4 %collective-permute-start.10 = (bf16[1536,128]{1,0:T(8,128)(2,1)S(1)}, bf16[1536,128]{1,0:T(8,128)(2,1)S(1)}, u32[]{:S(2)}, u32[]{:S(2)}) collective-permute-start(bf16[1536,128]{1,0:T(8,128)(2,1)S(1)} %get-tuple-element.30.refs_5_), channel_id=1, source_target_pairs={{0,8},{8,16},{16,24},{24,32},{32,40},{40,48},{48,56},{56,64},{64,7... | collective-permute-start | bytes 1179656 | tf_op jit(solution)/shard_map/ppermute | solution.py:391
  11.2 1.3 %collective-permute-start.3 = (bf16[3072,128]{1,0:T(8,128)(2,1)S(1)}, bf16[3072,128]{1,0:T(8,128)(2,1)S(1)}, u32[]{:S(2)}, u32[]{:S(2)}) collective-permute-start(bf16[3072,128]{1,0:T(8,128)(2,1)S(1)} %get-tuple-element.24), channel_id=1, source_target_pairs={{112,128},{140,124},{113,129},{141,125},{114,130},{142,126},{115,1... | collective-permute-start | bytes 2359304 | tf_op jit(solution)/shard_map/ppermute | solution.py:392
  12.5 2.8 %collective-permute-start.4 = (bf16[1536,128]{1,0:T(8,128)(2,1)S(1)}, bf16[1536,128]{1,0:T(8,128)(2,1)S(1)}, u32[]{:S(2)}, u32[]{:S(2)}) collective-permute-start(bf16[1536,128]{1,0:T(8,128)(2,1)S(1)} %get-tuple-element.25.refs_7_), channel_id=1, source_target_pairs={{0,8},{8,16},{16,24},{24,32},{32,40},{40,48},{48,56},{56,64},{64,7... | collective-permute-start | bytes 1179656 | tf_op jit(solution)/shard_map/ppermute | solution.py:391
  15.3 20.6 %collective-permute-done.10.refs_4_ = bf16[1536,128]{1,0:T(8,128)(2,1)S(1)} collective-permute-done((bf16[1536,128]{1,0:T(8,128)(2,1)S(1)}, bf16[1536,128]{1,0:T(8,128)(2,1)S(1)}, u32[]{:S(2)}, u32[]{:S(2)}) %collective-permute-start.10) | collective-permute-done | bytes 393248 | tf_op jit(solution)/shard_map/ppermute | solution.py:391
  35.9 1.3 %collective-permute-start.11 = (bf16[1536,128]{1,0:T(8,128)(2,1)S(1)}, bf16[1536,128]{1,0:T(8,128)(2,1)S(1)}, u32[]{:S(2)}, u32[]{:S(2)}) collective-permute-start(bf16[1536,128]{1,0:T(8,128)(2,1)S(1)} %collective-permute-done.10.refs_4_), channel_id=1, source_target_pairs={{0,8},{8,16},{16,24},{24,32},{32,40},{40,48},{48,56},{56,64},{64,7... | collective-permute-start | bytes 1179656 | tf_op jit(solution)/shard_map/ppermute | solution.py:393
  37.2 4.0 %collective-permute-done.4.refs_6_ = bf16[1536,128]{1,0:T(8,128)(2,1)S(1)} collective-permute-done((bf16[1536,128]{1,0:T(8,128)(2,1)S(1)}, bf16[1536,128]{1,0:T(8,128)(2,1)S(1)}, u32[]{:S(2)}, u32[]{:S(2)}) %collective-permute-start.4) | collective-permute-done | bytes 393248 | tf_op jit(solution)/shard_map/ppermute | solution.py:391
  41.2 1.3 %collective-permute-start.5 = (bf16[1536,128]{1,0:T(8,128)(2,1)S(1)}, bf16[1536,128]{1,0:T(8,128)(2,1)S(1)}, u32[]{:S(2)}, u32[]{:S(2)}) collective-permute-start(bf16[1536,128]{1,0:T(8,128)(2,1)S(1)} %collective-permute-done.4.refs_6_), channel_id=1, source_target_pairs={{0,8},{8,16},{16,24},{24,32},{32,40},{40,48},{48,56},{56,64},{64,7... | collective-permute-start | bytes 1179656 | tf_op jit(solution)/shard_map/ppermute | solution.py:393
  42.5 0.0 copy-start.4
  42.5 0.6 copy-done.4
  43.2 2.0 %shard_map.46 = (s32[6]{0:T(128)S(1)}, s32[3,1,256]{2,1,0:T(1,128)S(1)}) custom-call(s32[64]{0:T(128)S(1)} %copy-done.4), custom_call_target="tpu_custom_call" | custom-call | tf_op jit(solution)/shard_map/pallas_call | solution.py:318
  45.2 0.0 collective-permute-done.refs_3_
  45.2 0.0 copy-start
  45.2 1.5 %copy-done = bf16[768,1280]{1,0:T(8,128)(2,1)S(1)} copy-done((bf16[768,1280]{1,0:T(8,128)(2,1)S(1)}, bf16[768,1280]{1,0:T(8,128)(2,1)}, u32[]{:S(2)}) %copy-start) | copy-done | bytes 1966104
  46.8 8.8 %shard_map.49 = (bf16[768,640]{1,0:T(8,128)(2,1)S(1)}, f32[20,1,256]{2,1,0:T(1,128)S(1)}, f32[20,1,256]{2,1,0:T(1,128)S(1)}, f32[20,128,256]{2,1,0:T(8,128)S(1)}) custom-call(s32[6]{0:T(128)S(1)} %get-tuple-element.22.refs_0_, s32[3,1,256]{2,1,0:T(1,128)S(1)} %get-tuple-element.23.refs_1_, bf16[768,1280]{1,0:T(8,128)(2,1)S(1)} %copy-done, ...), custom_call_target="tpu_custom_call" | custom-call | tf_op jit(solution)/shard_map/pallas_call | solution.py:271
  55.6 0.0 collective-permute-done.11.refs_3_
  55.6 0.0 collective-permute-done.3.refs_4_.refs_2_
  55.6 0.0 copy-start.1
  55.6 5.9 %shard_map.50 = (bf16[192,640]{1,0:T(8,128)(2,1)S(1)}, bf16[192,640]{1,0:T(8,128)(2,1)S(1)}, bf16[192,640]{1,0:T(8,128)(2,1)S(1)}, bf16[192,640]{1,0:T(8,128)(2,...) custom-call(s32[6]{0:T(128)S(1)} %get-tuple-element.22.refs_0_, ...), custom_call_target="tpu_custom_call", output_to_operand_aliasing={{4}: (4, {}), {5}: (5, {}), {6}: (6, {}), {7}: (7, {})} | custom-call | tf_op jit(solution)/shard_map/pallas_call | solution.py:271
  61.5 0.7 collective-permute-start.12
  62.2 0.1 collective-permute-start.13
  62.2 4.3 %collective-permute-start.14 = (bf16[192,640]{1,0:T(8,128)(2,1)S(1)}, bf16[192,640]{1,0:T(8,128)(2,1)S(1)}, u32[]{:S(2)}, u32[]{:S(2)}) collective-permute-start(bf16[192,640]{1,0:T(8,128)(2,1)S(1)} %get-tuple-element.37), channel_id=1, source_target_pairs={{0,4},{1,5},{2,0},{3,1},{4,2},{5,3},{6,6},{7,7},{8,12},{9,13},{10,... | collective-permute-start | bytes 737288 | tf_op jit(solution)/shard_map/ppermute | solution.py:407
  66.5 0.0 collective-permute-done.5.refs_5_
  66.6 0.0 copy-done.1
  66.6 13.4 %shard_map.48 = (bf16[192,640]{1,0:T(8,128)(2,1)S(1)}, bf16[192,640]{1,0:T(8,128)(2,1)S(1)}, bf16[192,640]{1,0:T(8,128)(2,1)S(1)}, bf16[192,640]{1,0:T(8,128)(2,1)S(1)}) custom-call(s32[6]{0:T(128)S(1)} %get-tuple-element.22.refs_0_, s32[3,1,256]{2,1,0:T(1,128)S(1)} %get-tuple-element.23.refs_1_, bf16[768,1280]{1,0:T(8,128)(2,1)S(1)} %copy-done.1, ...), custom_call_target="tpu_custom_call" | custom-call | tf_op jit(solution)/shard_map/pallas_call | solution.py:271
  79.9 0.7 collective-permute-start.6
  80.6 0.1 collective-permute-start.7
  80.7 0.0 collective-permute-done.12.refs_0_
  80.7 2.0 %collective-permute-start.15 = (bf16[192,640]{1,0:T(8,128)(2,1)S(1)}, bf16[192,640]{1,0:T(8,128)(2,1)S(1)}, u32[]{:S(2)}, u32[]{:S(2)}) collective-permute-start(bf16[192,640]{1,0:T(8,128)(2,1)S(1)} %get-tuple-element.38), channel_id=1, source_target_pairs={{0,5},{1,0},{2,1},{3,4},{4,3},{5,6},{6,7},{7,2},{8,13},{9,8},{10,9... | collective-permute-start | bytes 737288 | tf_op jit(solution)/shard_map/ppermute | solution.py:407
  82.7 0.0 collective-permute-done.13.refs_1_
  82.7 2.5 %collective-permute-start.8 = (bf16[192,640]{1,0:T(8,128)(2,1)S(1)}, bf16[192,640]{1,0:T(8,128)(2,1)S(1)}, u32[]{:S(2)}, u32[]{:S(2)}) collective-permute-start(bf16[192,640]{1,0:T(8,128)(2,1)S(1)} %get-tuple-element.28), channel_id=1, source_target_pairs={{0,4},{1,5},{2,0},{3,1},{4,2},{5,3},{6,6},{7,7},{8,12},{9,13},{10,... | collective-permute-start | bytes 737288 | tf_op jit(solution)/shard_map/ppermute | solution.py:407
  85.3 0.0 collective-permute-done.14.refs_2_
  85.3 1.5 %collective-permute-start.9 = (bf16[192,640]{1,0:T(8,128)(2,1)S(1)}, bf16[192,640]{1,0:T(8,128)(2,1)S(1)}, u32[]{:S(2)}, u32[]{:S(2)}) collective-permute-start(bf16[192,640]{1,0:T(8,128)(2,1)S(1)} %get-tuple-element.29), channel_id=1, source_target_pairs={{0,5},{1,0},{2,1},{3,4},{4,3},{5,6},{6,7},{7,2},{8,13},{9,8},{10,9... | collective-permute-start | bytes 737288 | tf_op jit(solution)/shard_map/ppermute | solution.py:407
  86.8 18.3 %collective-permute-done.15.refs_3_ = bf16[192,640]{1,0:T(8,128)(2,1)S(1)} collective-permute-done((bf16[192,640]{1,0:T(8,128)(2,1)S(1)}, bf16[192,640]{1,0:T(8,128)(2,1)S(1)}, u32[]{:S(2)}, u32[]{:S(2)}) %collective-permute-start.15) | collective-permute-done | bytes 245792 | tf_op jit(solution)/shard_map/ppermute | solution.py:407
  105.0 1.0 shard_map.51.refs_4_
  106.0 0.0 collective-permute-done.6.refs_0_
  106.0 0.0 collective-permute-done.7.refs_1_
  106.0 0.0 collective-permute-done.8.refs_2_
  106.0 4.3 %collective-permute-done.9.refs_3_ = bf16[192,640]{1,0:T(8,128)(2,1)S(1)} collective-permute-done((bf16[192,640]{1,0:T(8,128)(2,1)S(1)}, bf16[192,640]{1,0:T(8,128)(2,1)S(1)}, u32[]{:S(2)}, u32[]{:S(2)}) %collective-permute-start.9) | collective-permute-done | bytes 245792 | tf_op jit(solution)/shard_map/ppermute | solution.py:407
  110.3 1.0 shard_map.52
  (1 shorter events, 0.0 us)
Async XLA Ops:
  0.0 45.2 %collective-permute-start = (bf16[768,1280]{1,0:T(8,128)(2,1)}, bf16[768,1280]{1,0:T(8,128)(2,1)S(1)}, u32[]{:S(2)}, u32[]{:S(2)}) collective-permute-start(bf16[768,1280]{1,0:T(8,128)(2,1)} %refs_2_.3), channel_id=1, source_target_pairs={{0,4},{4,0},{8,12},{12,8},{16,20},{20,16},{24,28},{28,24},{32,36},... | collective-permute-start | bytes 5898248 | tf_op jit(solution)/shard_map/ppermute | solution.py:387
  0.0 4.7 %collective-permute-start.1 = (bf16[768,256]{1,0:T(8,128)(2,1)}, bf16[768,256]{1,0:T(8,128)(2,1)S(1)}, u32[]{:S(2)}, u32[]{:S(2)}) collective-permute-start(bf16[768,256]{1,0:T(8,128)(2,1)} %k_ref.1), channel_id=1, source_target_pairs={{0,4},{4,0},{8,12},{12,8},{16,20},{20,16},{24,28},{28,24},{32,36},... | collective-permute-start | bytes 1179656 | tf_op jit(solution)/shard_map/ppermute | solution.py:385
  0.5 4.8 %collective-permute-start.2 = (bf16[768,256]{1,0:T(8,128)(2,1)}, bf16[768,256]{1,0:T(8,128)(2,1)S(1)}, u32[]{:S(2)}, u32[]{:S(2)}) collective-permute-start(bf16[768,256]{1,0:T(8,128)(2,1)} %v_ref.1), channel_id=1, source_target_pairs={{0,4},{4,0},{8,12},{12,8},{16,20},{20,16},{24,28},{28,24},{32,36},... | collective-permute-start | bytes 1179656 | tf_op jit(solution)/shard_map/ppermute | solution.py:386
  5.3 1.0 copy-start.2
  6.3 1.0 copy-start.3
  7.8 28.2 %collective-permute-start.10 = (bf16[1536,128]{1,0:T(8,128)(2,1)S(1)}, bf16[1536,128]{1,0:T(8,128)(2,1)S(1)}, u32[]{:S(2)}, u32[]{:S(2)}) collective-permute-start(bf16[1536,128]{1,0:T(8,128)(2,1)S(1)} %get-tuple-element.30.refs_5_), channel_id=1, source_target_pairs={{0,8},{8,16},{16,24},{24,32},{32,40},{40,48},{48,56},{56,64},{64,7... | collective-permute-start | bytes 1179656 | tf_op jit(solution)/shard_map/ppermute | solution.py:391
  11.2 44.4 %collective-permute-start.3 = (bf16[3072,128]{1,0:T(8,128)(2,1)S(1)}, bf16[3072,128]{1,0:T(8,128)(2,1)S(1)}, u32[]{:S(2)}, u32[]{:S(2)}) collective-permute-start(bf16[3072,128]{1,0:T(8,128)(2,1)S(1)} %get-tuple-element.24), channel_id=1, source_target_pairs={{112,128},{140,124},{113,129},{141,125},{114,130},{142,126},{115,1... | collective-permute-start | bytes 2359304 | tf_op jit(solution)/shard_map/ppermute | solution.py:392
  12.5 28.7 %collective-permute-start.4 = (bf16[1536,128]{1,0:T(8,128)(2,1)S(1)}, bf16[1536,128]{1,0:T(8,128)(2,1)S(1)}, u32[]{:S(2)}, u32[]{:S(2)}) collective-permute-start(bf16[1536,128]{1,0:T(8,128)(2,1)S(1)} %get-tuple-element.25.refs_7_), channel_id=1, source_target_pairs={{0,8},{8,16},{16,24},{24,32},{32,40},{40,48},{48,56},{56,64},{64,7... | collective-permute-start | bytes 1179656 | tf_op jit(solution)/shard_map/ppermute | solution.py:391
  35.9 19.6 %collective-permute-start.11 = (bf16[1536,128]{1,0:T(8,128)(2,1)S(1)}, bf16[1536,128]{1,0:T(8,128)(2,1)S(1)}, u32[]{:S(2)}, u32[]{:S(2)}) collective-permute-start(bf16[1536,128]{1,0:T(8,128)(2,1)S(1)} %collective-permute-done.10.refs_4_), channel_id=1, source_target_pairs={{0,8},{8,16},{16,24},{24,32},{32,40},{40,48},{48,56},{56,64},{64,7... | collective-permute-start | bytes 1179656 | tf_op jit(solution)/shard_map/ppermute | solution.py:393
  41.2 25.3 %collective-permute-start.5 = (bf16[1536,128]{1,0:T(8,128)(2,1)S(1)}, bf16[1536,128]{1,0:T(8,128)(2,1)S(1)}, u32[]{:S(2)}, u32[]{:S(2)}) collective-permute-start(bf16[1536,128]{1,0:T(8,128)(2,1)S(1)} %collective-permute-done.4.refs_6_), channel_id=1, source_target_pairs={{0,8},{8,16},{16,24},{24,32},{32,40},{40,48},{48,56},{56,64},{64,7... | collective-permute-start | bytes 1179656 | tf_op jit(solution)/shard_map/ppermute | solution.py:393
  42.5 0.7 copy-start.4
  45.2 1.5 %copy-start = (bf16[768,1280]{1,0:T(8,128)(2,1)S(1)}, bf16[768,1280]{1,0:T(8,128)(2,1)}, u32[]{:S(2)}) copy-start(bf16[768,1280]{1,0:T(8,128)(2,1)} %refs_2_.3) | copy-start | bytes 5898244
  55.6 11.0 %copy-start.1 = (bf16[768,1280]{1,0:T(8,128)(2,1)S(1)}, bf16[768,1280]{1,0:T(8,128)(2,1)}, u32[]{:S(2)}) copy-start(bf16[768,1280]{1,0:T(8,128)(2,1)} %refs_2_.3) | copy-start | bytes 5898244
  61.5 19.2 %collective-permute-start.12 = (bf16[192,640]{1,0:T(8,128)(2,1)S(1)}, bf16[192,640]{1,0:T(8,128)(2,1)S(1)}, u32[]{:S(2)}, u32[]{:S(2)}) collective-permute-start(bf16[192,640]{1,0:T(8,128)(2,1)S(1)} %get-tuple-element.35), channel_id=1, source_target_pairs={{0,0},{1,1},{2,4},{3,5},{4,6},{5,7},{6,2},{7,3},{8,8},{9,9},{10,12... | collective-permute-start | bytes 737288 | tf_op jit(solution)/shard_map/ppermute | solution.py:407
  62.2 20.6 %collective-permute-start.13 = (bf16[192,640]{1,0:T(8,128)(2,1)S(1)}, bf16[192,640]{1,0:T(8,128)(2,1)S(1)}, u32[]{:S(2)}, u32[]{:S(2)}) collective-permute-start(bf16[192,640]{1,0:T(8,128)(2,1)S(1)} %get-tuple-element.36), channel_id=1, source_target_pairs={{0,1},{1,4},{2,5},{3,0},{4,7},{5,2},{6,3},{7,6},{8,9},{9,12},{10,1... | collective-permute-start | bytes 737288 | tf_op jit(solution)/shard_map/ppermute | solution.py:407
  62.2 23.0 %collective-permute-start.14 = (bf16[192,640]{1,0:T(8,128)(2,1)S(1)}, bf16[192,640]{1,0:T(8,128)(2,1)S(1)}, u32[]{:S(2)}, u32[]{:S(2)}) collective-permute-start(bf16[192,640]{1,0:T(8,128)(2,1)S(1)} %get-tuple-element.37), channel_id=1, source_target_pairs={{0,4},{1,5},{2,0},{3,1},{4,2},{5,3},{6,6},{7,7},{8,12},{9,13},{10,... | collective-permute-start | bytes 737288 | tf_op jit(solution)/shard_map/ppermute | solution.py:407
  79.9 26.1 %collective-permute-start.6 = (bf16[192,640]{1,0:T(8,128)(2,1)S(1)}, bf16[192,640]{1,0:T(8,128)(2,1)S(1)}, u32[]{:S(2)}, u32[]{:S(2)}) collective-permute-start(bf16[192,640]{1,0:T(8,128)(2,1)S(1)} %get-tuple-element.26), channel_id=1, source_target_pairs={{0,0},{1,1},{2,4},{3,5},{4,6},{5,7},{6,2},{7,3},{8,8},{9,9},{10,12... | collective-permute-start | bytes 737288 | tf_op jit(solution)/shard_map/ppermute | solution.py:407
  80.6 25.4 %collective-permute-start.7 = (bf16[192,640]{1,0:T(8,128)(2,1)S(1)}, bf16[192,640]{1,0:T(8,128)(2,1)S(1)}, u32[]{:S(2)}, u32[]{:S(2)}) collective-permute-start(bf16[192,640]{1,0:T(8,128)(2,1)S(1)} %get-tuple-element.27), channel_id=1, source_target_pairs={{0,1},{1,4},{2,5},{3,0},{4,7},{5,2},{6,3},{7,6},{8,9},{9,12},{10,1... | collective-permute-start | bytes 737288 | tf_op jit(solution)/shard_map/ppermute | solution.py:407
  80.7 24.3 %collective-permute-start.15 = (bf16[192,640]{1,0:T(8,128)(2,1)S(1)}, bf16[192,640]{1,0:T(8,128)(2,1)S(1)}, u32[]{:S(2)}, u32[]{:S(2)}) collective-permute-start(bf16[192,640]{1,0:T(8,128)(2,1)S(1)} %get-tuple-element.38), channel_id=1, source_target_pairs={{0,5},{1,0},{2,1},{3,4},{4,3},{5,6},{6,7},{7,2},{8,13},{9,8},{10,9... | collective-permute-start | bytes 737288 | tf_op jit(solution)/shard_map/ppermute | solution.py:407
  82.7 23.3 %collective-permute-start.8 = (bf16[192,640]{1,0:T(8,128)(2,1)S(1)}, bf16[192,640]{1,0:T(8,128)(2,1)S(1)}, u32[]{:S(2)}, u32[]{:S(2)}) collective-permute-start(bf16[192,640]{1,0:T(8,128)(2,1)S(1)} %get-tuple-element.28), channel_id=1, source_target_pairs={{0,4},{1,5},{2,0},{3,1},{4,2},{5,3},{6,6},{7,7},{8,12},{9,13},{10,... | collective-permute-start | bytes 737288 | tf_op jit(solution)/shard_map/ppermute | solution.py:407
  85.3 25.0 %collective-permute-start.9 = (bf16[192,640]{1,0:T(8,128)(2,1)S(1)}, bf16[192,640]{1,0:T(8,128)(2,1)S(1)}, u32[]{:S(2)}, u32[]{:S(2)}) collective-permute-start(bf16[192,640]{1,0:T(8,128)(2,1)S(1)} %get-tuple-element.29), channel_id=1, source_target_pairs={{0,5},{1,0},{2,1},{3,4},{4,3},{5,6},{6,7},{7,2},{8,13},{9,8},{10,9... | collective-permute-start | bytes 737288 | tf_op jit(solution)/shard_map/ppermute | solution.py:407
